TPU v7x, 32 devices: a whole 2x2x4 slice. The times are simulated.
32 devices in a mesh: rows: 4 (over y, core), cols: 8 (over z, x).
Axes of the slice: x: 2, y: 2, z: 4, core: 2. Of those that a mesh axis runs over, the one named last changes fastest.
Arguments:
- terrain_grid: float32 [4096, 4096], P('rows', 'cols'), may hold values from -360 to 360
Outputs:
- shade: float32 [4096, 4096], P('rows', 'cols')
- first: float32 [2048, 2048], P('rows', 'cols')
- second: float32 [1024, 1024], P('rows', 'cols')
- third: float32 [512, 512], P('rows', 'cols')
All inputs are finite; a program needn't handle non-finite values.
Results may differ from a plain program's by a relative error of at most 0.0003.
Values sent between devices are 32-bit elements; how exact they have to be, the bound alone decides.
A program may use at most 64 MiB of HBM per device.

v0:
```python
import math

import jax
import jax.numpy as jnp
from jax import lax
from jax.experimental import pallas as pl
from jax.experimental.pallas import tpu as pltpu
from jax.sharding import PartitionSpec as P

REACH = 120
HALO = 128
LANES = 128
STEPS = 2 * REACH // 8
LIGHT_UP = math.sqrt(0.5)


def rolled(x, k):
    return pltpu.roll(x, x.shape[0] - k, 0)


def group_extremes(load_hi, load_lo, out_hi, out_lo, rows):
    size = 128

    def body(c, carry):
        r = pl.multiple_of(c * size, size)
        top = load_hi(r, size + 8)
        if load_lo is None:
            after = rolled(top, 1)
            hi, lo = jnp.maximum(top, after), jnp.minimum(top, after)
        else:
            low = load_lo(r, size + 8)
            hi, lo = jnp.maximum(top, rolled(top, 1)), jnp.minimum(low, rolled(low, 1))
        for k in (2, 4):
            hi = jnp.maximum(hi, rolled(hi, k))
            lo = jnp.minimum(lo, rolled(lo, k))
        out_hi[pl.ds(r, size), :] = hi[:size]
        out_lo[pl.ds(r, size), :] = lo[:size]
        return carry

    lax.fori_loop(0, rows // size, body, 0)


def window_chunk(load, last, pick, groups):
    held = [None] * groups
    run = load(groups - 1)
    for k in range(groups, STEPS):
        run = pick(run, load(k))
    held[groups - 1] = run
    for g in range(groups - 2, -1, -1):
        run = pick(run, load(g))
        held[g] = run
    out = [pick(held[0], last(STEPS))]
    run = None
    for g in range(1, groups):
        nxt = load(g + STEPS - 1)
        run = nxt if run is None else pick(run, nxt)
        out.append(pick(pick(held[g], run), last(g + STEPS)))
    return out


def chunking(groups):
    return max(g for g in range(1, STEPS) if groups % g == 0)


def vertical_pass(x, vhi, vlo, mhi, mlo, b, rows):
    load = lambda r, n: x[b, pl.ds(r, n), :]
    group_extremes(load, None, mhi, mlo, rows + 2 * HALO)
    total = (rows + 16) // 8
    size = chunking(total)

    def body(c, carry):
        base = c * size
        last = lambda k: x[b, pl.ds(pl.multiple_of((base + k) * 8, 8), 8), :]
        for m, v, pick in ((mhi, vhi, jnp.maximum), (mlo, vlo, jnp.minimum)):
            load = lambda k: m[pl.ds(pl.multiple_of((base + k) * 8, 8), 8), :]
            for g, value in enumerate(window_chunk(load, last, pick, size)):
                v[b, pl.ds(pl.multiple_of((base + g) * 8, 8), 8), :] = value
        return carry

    lax.fori_loop(0, total // size, body, 0)


def horizontal_pass(x, vhi, vlo, relief, thi, tlo, mhi, mlo, mid, rb, strips):
    width = strips * LANES
    r = pl.multiple_of(rb * LANES, LANES)
    for b in range(strips):
        thi[b * LANES : (b + 1) * LANES, :] = vhi[b, pl.ds(r, LANES), :].T
        tlo[b * LANES : (b + 1) * LANES, :] = vlo[b, pl.ds(r, LANES), :].T
    group_extremes(
        lambda s, n: thi[pl.ds(s, n), :], lambda s, n: tlo[pl.ds(s, n), :], mhi, mlo, width
    )
    total = (width - 2 * HALO + 16) // 8
    size = chunking(total)

    def body(c, carry):
        base = c * size
        at = lambda ref: (lambda k: ref[pl.ds(pl.multiple_of((base + k) * 8, 8), 8), :])
        highest = window_chunk(at(mhi), at(thi), jnp.maximum, size)
        lowest = window_chunk(at(mlo), at(tlo), jnp.minimum, size)
        for g in range(size):
            mid[pl.ds(pl.multiple_of(REACH + (base + g) * 8, 8), 8), :] = (
                highest[g] + lowest[g]
            ) * 0.5
        return carry

    lax.fori_loop(0, total // size, body, 0)
    q = pl.multiple_of(r + REACH, 8)
    for b in range(strips):
        relief[b, pl.ds(q, LANES), :] = (
            x[b, pl.ds(q, LANES), :] - mid[b * LANES : (b + 1) * LANES, :].T
        )


def repair(ref, strips, first_row, rows, low, high, edges):
    top, bottom, left, right = edges

    @pl.when(top)
    def _():
        for b in range(strips):
            ref[b, first_row - 8 : first_row, :] = jnp.broadcast_to(
                ref[b, first_row : first_row + 1, :], (8, LANES)
            )

    @pl.when(bottom)
    def _():
        end = first_row + rows
        for b in range(strips):
            ref[b, end : end + 8, :] = jnp.broadcast_to(ref[b, end - 1 : end, :], (8, LANES))

    @pl.when(left)
    def _():
        ref[0, low:high, :] = jnp.broadcast_to(ref[1, low:high, 0:1], (high - low, LANES))

    @pl.when(right)
    def _():
        ref[strips - 1, low:high, :] = jnp.broadcast_to(
            ref[strips - 2, low:high, LANES - 1 : LANES], (high - low, LANES)
        )


def shade_rows(relief, shade, strips, rows):
    size = 16
    width = strips * LANES

    def body(c, carry):
        r = pl.multiple_of(HALO - 16 + c * size, 8)
        wide = jnp.concatenate(
            [relief[b, pl.ds(r - 8, size + 16), :] for b in range(strips)], axis=1
        )
        north = pltpu.roll(wide, 1, 0)[8 : 8 + size]
        south = pltpu.roll(wide, size + 15, 0)[8 : 8 + size]
        here = wide[8 : 8 + size]
        across = north + 2.0 * here + south
        down = south - north
        gx = (pltpu.roll(across, width - 1, 1) - pltpu.roll(across, 1, 1)) * 0.25
        gy = (pltpu.roll(down, width - 1, 1) + 2.0 * down + pltpu.roll(down, 1, 1)) * 0.25
        lit = (LIGHT_UP + 0.5 * gx + 0.5 * gy) * lax.rsqrt(1.0 + gx * gx + gy * gy)
        lit = jnp.maximum(lit, 0.0)
        for b in range(strips):
            shade[b, pl.ds(r, size), :] = lit[:, b * LANES : (b + 1) * LANES]
        return carry

    lax.fori_loop(0, (rows + 32) // size, body, 0)


def tent_matrix(d):
    row = lax.broadcasted_iota(jnp.int32, (LANES, LANES), 0)
    col = lax.broadcasted_iota(jnp.int32, (LANES, LANES), 1)
    t = row + d * LANES - 2 * col + LANES
    near, far = (t == 0) | (t == 1), (t == -1) | (t == 2)
    return jnp.where(near, 0.375, jnp.where(far, 0.125, 0.0)).astype(jnp.bfloat16)


def next_level(source, strips, start, count, outs, uhi, ulo, store):
    def body(b, carry):
        at = lambda k: source[b, pl.ds(2 * start + k, count, stride=2), :]
        u = (at(-1) + at(2)) * 0.125 + (at(0) + at(1)) * 0.375
        upper = u.astype(jnp.bfloat16)
        uhi[b, 0:count, :] = upper
        ulo[b, 0:count, :] = (u - upper.astype(jnp.float32)).astype(jnp.bfloat16)
        return carry

    lax.fori_loop(0, strips, body, 0)
    tents = {d: tent_matrix(d) for d in (-2, -1, 0, 1)}
    for out in outs:
        parts = [b for b in range(2 * out - 2, 2 * out + 2) if 0 <= b < strips]
        weights = jnp.concatenate([tents[b - 2 * out] for b in parts], axis=0)
        total = None
        for u in (uhi, ulo):
            left = jnp.concatenate([u[b, 0:count, :] for b in parts], axis=1)
            term = jnp.dot(left, weights, preferred_element_type=jnp.float32)
            total = term if total is None else total + term
        store(out, total)


def kernel(
    own, left, right, top, bottom, out_shade, out_first, out_second, out_third,
    x, vhi, vlo, relief, shade, first, second, thi, tlo, mhi, mlo, mid, uhi, ulo, sems,
):
    rows, cols = own.shape
    strips = cols // LANES + 2
    i, ni = lax.axis_index("rows"), lax.axis_size("rows")
    j, nj = lax.axis_index("cols"), lax.axis_size("cols")
    edges = (i == 0, i == ni - 1, j == 0, j == nj - 1)
    mine = pl.ds(HALO, rows)
    copies = []
    for b in range(strips - 2):
        copies.append((own.at[:, pl.ds(b * LANES, LANES)], x.at[b + 1, mine, :]))
    copies.append((left, x.at[0, mine, :]))
    copies.append((right, x.at[strips - 1, mine, :]))
    for b in range(strips):
        lanes = pl.ds(b * LANES, LANES)
        copies.append((top.at[:, lanes], x.at[b, pl.ds(0, HALO), :]))
        copies.append((bottom.at[:, lanes], x.at[b, pl.ds(HALO + rows, HALO), :]))
    started = [pltpu.make_async_copy(s, d, sems.at[n]) for n, (s, d) in enumerate(copies)]
    for copy in started:
        copy.start()
    mid[...] = jnp.zeros_like(mid)
    for copy in started:
        copy.wait()

    @pl.when(edges[2])
    def _():
        x[0, 0 : rows + 2 * HALO, :] = jnp.broadcast_to(
            x[1, 0 : rows + 2 * HALO, 0:1], (rows + 2 * HALO, LANES)
        )

    @pl.when(edges[3])
    def _():
        x[strips - 1, 0 : rows + 2 * HALO, :] = jnp.broadcast_to(
            x[strips - 2, 0 : rows + 2 * HALO, LANES - 1 : LANES], (rows + 2 * HALO, LANES)
        )

    @pl.when(edges[0])
    def _():
        for b in range(strips):
            x[b, 0:HALO, :] = jnp.broadcast_to(x[b, HALO : HALO + 1, :], (HALO, LANES))

    @pl.when(edges[1])
    def _():
        end = HALO + rows
        for b in range(strips):
            x[b, end : end + HALO, :] = jnp.broadcast_to(x[b, end - 1 : end, :], (HALO, LANES))

    def down(b, carry):
        vertical_pass(x, vhi, vlo, mhi, mlo, b, rows)
        return carry

    lax.fori_loop(0, strips, down, 0)

    def along(rb, carry):
        horizontal_pass(x, vhi, vlo, relief, thi, tlo, mhi, mlo, mid, rb, strips)
        return carry

    lax.fori_loop(0, rows // LANES + 1, along, 0)

    repair(relief, strips, HALO, rows, HALO - 8, HALO + rows + 8, edges)
    shade_rows(relief, shade, strips, rows)
    repair(shade, strips, HALO, rows, HALO - 8, HALO + rows + 8, edges)
    outgoing = []

    def send(source, target):
        copy = pltpu.make_async_copy(source, target, sems.at[len(outgoing)])
        copy.start()
        outgoing.append(copy)

    for b in range(strips - 2):
        send(shade.at[b + 1, mine, :], out_shade.at[:, pl.ds(b * LANES, LANES)])

    half, quarter = HALO // 2, HALO // 4
    strips1 = cols // 256 + 2
    low = half - 8

    def keep_first(out, value):
        first[out, low : low + rows // 2 + 16, :] = value

    next_level(shade, strips, low, rows // 2 + 16, range(strips1), uhi, ulo, keep_first)
    repair(first, strips1, half, rows // 2, low, low + rows // 2 + 16, edges)
    for b in range(strips1 - 2):
        send(
            first.at[b + 1, pl.ds(half, rows // 2), :],
            out_first.at[:, pl.ds(b * LANES, LANES)],
        )
    strips2 = cols // 512 + 2
    low2 = quarter - 8

    def keep_second(out, value):
        second[out, low2 : low2 + rows // 4 + 16, :] = value

    next_level(first, strips1, low2, rows // 4 + 16, range(strips2), uhi, ulo, keep_second)
    repair(second, strips2, quarter, rows // 4, low2, low2 + rows // 4 + 16, edges)
    for b in range(strips2 - 2):
        send(
            second.at[b + 1, pl.ds(quarter, rows // 4), :],
            out_second.at[:, pl.ds(b * LANES, LANES)],
        )

    def keep_third(out, value):
        n = min(LANES, cols // 8 - (out - 1) * LANES)
        out_third[:, (out - 1) * LANES : (out - 1) * LANES + n] = value[:, :n]

    outs3 = range(1, 1 + -(-cols // 1024))
    next_level(second, strips2, HALO // 8, rows // 8, outs3, uhi, ulo, keep_third)
    for copy in outgoing:
        copy.wait()


def shifted(array, axis, by):
    count = lax.axis_size(axis)
    pairs = [(k, k + by) for k in range(count) if 0 <= k + by < count]
    return lax.ppermute(array, axis, pairs)


def on_device(terrain):
    rows, cols = terrain.shape
    strips = cols // LANES + 2
    left = shifted(terrain[:, cols - HALO :], "cols", 1)
    right = shifted(terrain[:, :HALO], "cols", -1)
    top_mine = shifted(terrain[rows - HALO :], "rows", 1)
    bottom_mine = shifted(terrain[:HALO], "rows", -1)
    ends = jnp.concatenate([left[rows - HALO :], right[rows - HALO :]], axis=1)
    starts = jnp.concatenate([left[:HALO], right[:HALO]], axis=1)
    top_ends = shifted(ends, "rows", 1)
    bottom_ends = shifted(starts, "rows", -1)
    top = jnp.concatenate([top_ends[:, :LANES], top_mine, top_ends[:, LANES:]], axis=1)
    bottom = jnp.concatenate([bottom_ends[:, :LANES], bottom_mine, bottom_ends[:, LANES:]], axis=1)
    f32 = jnp.float32
    tall = rows + 2 * HALO + 8
    anywhere = pl.BlockSpec(memory_space=pl.ANY)
    vmem = pl.BlockSpec(memory_space=pltpu.VMEM)
    return pl.pallas_call(
        kernel,
        out_shape=tuple(
            jax.ShapeDtypeStruct((rows // k, cols // k), f32) for k in (1, 2, 4, 8)
        ),
        in_specs=[anywhere] * 5,
        out_specs=(anywhere, anywhere, anywhere, vmem),
        scratch_shapes=[
            pltpu.VMEM((strips, tall, LANES), f32),
            pltpu.VMEM((strips, rows + LANES, LANES), f32),
            pltpu.VMEM((strips, rows + LANES, LANES), f32),
            pltpu.VMEM((strips, tall, LANES), f32),
            pltpu.VMEM((strips, tall, LANES), f32),
            pltpu.VMEM((cols // 256 + 2, rows // 2 + HALO, LANES), f32),
            pltpu.VMEM((cols // 512 + 2, rows // 4 + HALO, LANES), f32),
            pltpu.VMEM((strips * LANES + 8, LANES), f32),
            pltpu.VMEM((strips * LANES + 8, LANES), f32),
            pltpu.VMEM((max(tall, strips * LANES), LANES), f32),
            pltpu.VMEM((max(tall, strips * LANES), LANES), f32),
            pltpu.VMEM((strips * LANES, LANES), f32),
            pltpu.VMEM((strips, rows // 2 + 16, LANES), jnp.bfloat16),
            pltpu.VMEM((strips, rows // 2 + 16, LANES), jnp.bfloat16),
            pltpu.SemaphoreType.DMA((3 * strips + 8,)),
        ],
        compiler_params=pltpu.CompilerParams(vmem_limit_bytes=58 * 1024 * 1024),
    )(terrain, left, right, top, bottom)


def solution(mesh):
    spec = P("rows", "cols")
    return jax.shard_map(
        on_device, mesh=mesh, in_specs=(spec,), out_specs=(spec,) * 4, check_vma=False
    )
```

profile of v0, /device:TPU:19, one launch (start us, length us, event | category | flops | bytes accessed | tf_op | source)
XLA Modules:
  0.0 75.8 jit_solution(17184415397148655449)
XLA Ops:
  0.6 1.3 %fusion.1 = (f32[1024,128]{1,0:T(8,128)S(1)}, f32[1024,128]{1,0:T(8,128)S(1)}) fusion(f32[1024,512]{1,0:T(8,128)} %own.1), kind=kLoop, calls=%fused_computation.5 | loop fusion | bytes 2097152 | tf_op jit(solution)/shard_map/slice | solution.py:318
  1.9 2.2 %collective-permute-start.1 = (f32[1024,128]{1,0:T(8,128)S(1)}, f32[1024,128]{1,0:T(8,128)S(1)}, u32[]{:S(2)}, u32[]{:S(2)}) collective-permute-start(f32[1024,128]{1,0:T(8,128)S(1)} %get-tuple-element.10), channel_id=1, source_target_pairs={{1,0},{2,1},{3,2},{4,3},{5,4},{6,5},{7,6},{9,8},{10,9},{11,10},{12... | collective-permute-start | bytes 1572872 | tf_op jit(solution)/shard_map/ppermute | solution.py:311
  4.1 4.0 %collective-permute-start = (f32[1024,128]{1,0:T(8,128)S(1)}, f32[1024,128]{1,0:T(8,128)S(1)}, u32[]{:S(2)}, u32[]{:S(2)}) collective-permute-start(f32[1024,128]{1,0:T(8,128)S(1)} %get-tuple-element.11), channel_id=1, source_target_pairs={{0,1},{1,2},{2,3},{3,4},{4,5},{5,6},{6,7},{8,9},{9,10},{10,11},{11... | collective-permute-start | bytes 1572872 | tf_op jit(solution)/shard_map/ppermute | solution.py:311
  8.1 17.8 %collective-permute-done.1.right = f32[1024,128]{1,0:T(8,128)S(1)} collective-permute-done((f32[1024,128]{1,0:T(8,128)S(1)}, f32[1024,128]{1,0:T(8,128)S(1)}, u32[]{:S(2)}, u32[]{:S(2)}) %collective-permute-start.1) | collective-permute-done | bytes 524320 | tf_op jit(solution)/shard_map/ppermute | solution.py:311
  25.9 0.0 copy-start
  25.9 3.9 %collective-permute-done.left = f32[1024,128]{1,0:T(8,128)S(1)} collective-permute-done((f32[1024,128]{1,0:T(8,128)S(1)}, f32[1024,128]{1,0:T(8,128)S(1)}, u32[]{:S(2)}, u32[]{:S(2)}) %collective-permute-start) | collective-permute-done | bytes 524320 | tf_op jit(solution)/shard_map/ppermute | solution.py:311
  29.8 0.0 copy-start.1
  29.8 3.5 %collective-permute-start.2 = (f32[128,256]{1,0:T(8,128)S(1)}, f32[128,256]{1,0:T(8,128)S(1)}, u32[]{:S(2)}, u32[]{:S(2)}) collective-permute-start(f32[128,256]{1,0:T(8,128)S(1)} %pad_maximum_fusion.2), channel_id=1, source_target_pairs={{0,8},{8,16},{16,24},{1,9},{9,17},{17,25},{2,10},{10,18},{18,26},{... | collective-permute-start | bytes 393224 | tf_op jit(solution)/shard_map/ppermute | solution.py:311
  33.4 1.1 %fusion = (f32[128,512]{1,0:T(8,128)S(1)}, f32[128,512]{1,0:T(8,128)S(1)}) fusion(f32[1024,512]{1,0:T(8,128)} %own.1), kind=kLoop, calls=%fused_computation.4 | loop fusion | bytes 1048576 | tf_op jit(solution)/shard_map/slice | solution.py:320
  34.4 1.9 %collective-permute-start.5 = (f32[128,512]{1,0:T(8,128)S(1)}, f32[128,512]{1,0:T(8,128)S(1)}, u32[]{:S(2)}, u32[]{:S(2)}) collective-permute-start(f32[128,512]{1,0:T(8,128)S(1)} %get-tuple-element.8), channel_id=1, source_target_pairs={{8,0},{16,8},{24,16},{9,1},{17,9},{25,17},{10,2},{18,10},{26,18},{... | collective-permute-start | bytes 786440 | tf_op jit(solution)/shard_map/ppermute | solution.py:311
  36.4 3.6 %collective-permute-start.3 = (f32[128,512]{1,0:T(8,128)S(1)}, f32[128,512]{1,0:T(8,128)S(1)}, u32[]{:S(2)}, u32[]{:S(2)}) collective-permute-start(f32[128,512]{1,0:T(8,128)S(1)} %get-tuple-element.9), channel_id=1, source_target_pairs={{0,8},{8,16},{16,24},{1,9},{9,17},{17,25},{2,10},{10,18},{18,26},{... | collective-permute-start | bytes 786440 | tf_op jit(solution)/shard_map/ppermute | solution.py:311
  40.0 1.9 %collective-permute-start.4 = (f32[128,256]{1,0:T(8,128)S(1)}, f32[128,256]{1,0:T(8,128)S(1)}, u32[]{:S(2)}, u32[]{:S(2)}) collective-permute-start(f32[128,256]{1,0:T(8,128)S(1)} %pad_maximum_fusion.3), channel_id=1, source_target_pairs={{8,0},{16,8},{24,16},{9,1},{17,9},{25,17},{10,2},{18,10},{26,18},{... | collective-permute-start | bytes 393224 | tf_op jit(solution)/shard_map/ppermute | solution.py:311
  41.9 0.0 collective-permute-done.2
  42.0 1.3 %collective-permute-done.3 = f32[128,512]{1,0:T(8,128)S(1)} collective-permute-done((f32[128,512]{1,0:T(8,128)S(1)}, f32[128,512]{1,0:T(8,128)S(1)}, u32[]{:S(2)}, u32[]{:S(2)}) %collective-permute-start.3) | collective-permute-done | bytes 262176 | tf_op jit(solution)/shard_map/ppermute | solution.py:311
  43.3 0.8 %pad_maximum_fusion.top = f32[128,768]{1,0:T(8,128)} fusion(f32[128,128]{1,0:T(8,128)S(1)} %get-tuple-element.19, f32[128,512]{1,0:T(8,128)S(1)} %collective-permute-done.3, f32[128,128]{1,0:T(8,128)S(1)} %get-tuple-element.18), kind=kLoop, calls=%fused_computation | loop fusion | flops 196608 | bytes 786432 | tf_op jit(solution)/shard_map/concatenate | solution.py:325
  44.1 2.2 %collective-permute-done.4 = f32[128,256]{1,0:T(8,128)S(1)} collective-permute-done((f32[128,256]{1,0:T(8,128)S(1)}, f32[128,256]{1,0:T(8,128)S(1)}, u32[]{:S(2)}, u32[]{:S(2)}) %collective-permute-start.4) | collective-permute-done | bytes 131104 | tf_op jit(solution)/shard_map/ppermute | solution.py:311
  46.3 0.0 collective-permute-done.5
  46.3 0.8 %pad_maximum_fusion.1.bottom = f32[128,768]{1,0:T(8,128)} fusion(f32[128,128]{1,0:T(8,128)S(1)} %get-tuple-element.17, f32[128,512]{1,0:T(8,128)S(1)} %collective-permute-done.5, f32[128,128]{1,0:T(8,128)S(1)} %get-tuple-element.16), kind=kLoop, calls=%fused_computation.1 | loop fusion | flops 196608 | bytes 786432 | tf_op jit(solution)/shard_map/concatenate | solution.py:326
  47.1 0.0 copy-done
  47.1 0.0 copy-done.1
  47.1 27.1 %shard_map.46 = (f32[1024,512]{1,0:T(8,128)}, f32[512,256]{1,0:T(8,128)}, f32[256,128]{1,0:T(8,128)}, f32[128,64]{1,0:T(8,128)}) custom-call(f32[1024,512]{1,0:T(8,128)} %own.1, f32[1024,128]{1,0:T(8,128)} %copy-done.1, f32[1024,128]{1,0:T(8,128)} %copy-done, f32[128,768]{1,0:T(8,128)} %pad_maximum_fusion.top, f32[128,768]{1,0:T(8,128)} %pad_maximum_fusion.1.bottom), custom_call_target="tpu_custom_call" | custom-call | tf_op jit(solution)/shard_map/pallas_call | solution.py:331
  74.3 1.5 %copy.5 = f32[128,64]{0,1:T(8,128)} copy(f32[128,64]{1,0:T(8,128)} %get-tuple-element.7) | data formatting | bytes 65536 | tf_op jit(solution)/shard_map/pallas_call | solution.py:331
  (6 shorter events, 0.1 us)
Async XLA Ops:
  1.9 24.0 %collective-permute-start.1 = (f32[1024,128]{1,0:T(8,128)S(1)}, f32[1024,128]{1,0:T(8,128)S(1)}, u32[]{:S(2)}, u32[]{:S(2)}) collective-permute-start(f32[1024,128]{1,0:T(8,128)S(1)} %get-tuple-element.10), channel_id=1, source_target_pairs={{1,0},{2,1},{3,2},{4,3},{5,4},{6,5},{7,6},{9,8},{10,9},{11,10},{12... | collective-permute-start | bytes 1572872 | tf_op jit(solution)/shard_map/ppermute | solution.py:311
  4.1 25.7 %collective-permute-start = (f32[1024,128]{1,0:T(8,128)S(1)}, f32[1024,128]{1,0:T(8,128)S(1)}, u32[]{:S(2)}, u32[]{:S(2)}) collective-permute-start(f32[1024,128]{1,0:T(8,128)S(1)} %get-tuple-element.11), channel_id=1, source_target_pairs={{0,1},{1,2},{2,3},{3,4},{4,5},{5,6},{6,7},{8,9},{9,10},{10,11},{11... | collective-permute-start | bytes 1572872 | tf_op jit(solution)/shard_map/ppermute | solution.py:311
  25.9 21.2 %copy-start = (f32[1024,128]{1,0:T(8,128)}, f32[1024,128]{1,0:T(8,128)S(1)}, u32[]{:S(2)}) copy-start(f32[1024,128]{1,0:T(8,128)S(1)} %collective-permute-done.1.right) | copy-start | bytes 1572868
  29.8 17.3 %copy-start.1 = (f32[1024,128]{1,0:T(8,128)}, f32[1024,128]{1,0:T(8,128)S(1)}, u32[]{:S(2)}) copy-start(f32[1024,128]{1,0:T(8,128)S(1)} %collective-permute-done.left) | copy-start | bytes 1572868
  29.8 12.1 %collective-permute-start.2 = (f32[128,256]{1,0:T(8,128)S(1)}, f32[128,256]{1,0:T(8,128)S(1)}, u32[]{:S(2)}, u32[]{:S(2)}) collective-permute-start(f32[128,256]{1,0:T(8,128)S(1)} %pad_maximum_fusion.2), channel_id=1, source_target_pairs={{0,8},{8,16},{16,24},{1,9},{9,17},{17,25},{2,10},{10,18},{18,26},{... | collective-permute-start | bytes 393224 | tf_op jit(solution)/shard_map/ppermute | solution.py:311
  34.4 11.9 %collective-permute-start.5 = (f32[128,512]{1,0:T(8,128)S(1)}, f32[128,512]{1,0:T(8,128)S(1)}, u32[]{:S(2)}, u32[]{:S(2)}) collective-permute-start(f32[128,512]{1,0:T(8,128)S(1)} %get-tuple-element.8), channel_id=1, source_target_pairs={{8,0},{16,8},{24,16},{9,1},{17,9},{25,17},{10,2},{18,10},{26,18},{... | collective-permute-start | bytes 786440 | tf_op jit(solution)/shard_map/ppermute | solution.py:311
  36.4 6.9 %collective-permute-start.3 = (f32[128,512]{1,0:T(8,128)S(1)}, f32[128,512]{1,0:T(8,128)S(1)}, u32[]{:S(2)}, u32[]{:S(2)}) collective-permute-start(f32[128,512]{1,0:T(8,128)S(1)} %get-tuple-element.9), channel_id=1, source_target_pairs={{0,8},{8,16},{16,24},{1,9},{9,17},{17,25},{2,10},{10,18},{18,26},{... | collective-permute-start | bytes 786440 | tf_op jit(solution)/shard_map/ppermute | solution.py:311
  40.0 6.3 %collective-permute-start.4 = (f32[128,256]{1,0:T(8,128)S(1)}, f32[128,256]{1,0:T(8,128)S(1)}, u32[]{:S(2)}, u32[]{:S(2)}) collective-permute-start(f32[128,256]{1,0:T(8,128)S(1)} %pad_maximum_fusion.3), channel_id=1, source_target_pairs={{8,0},{16,8},{24,16},{9,1},{17,9},{25,17},{10,2},{18,10},{26,18},{... | collective-permute-start | bytes 393224 | tf_op jit(solution)/shard_map/ppermute | solution.py:311
where the time goes:
time: 76.9 us; the launch traced here: 75.8 us
  Pallas kernels  27.1 us (35%)
  waiting for transfers between devices  25.2 us (33%)
  starting transfers between devices  17.2 us (22%)
  local copies, waits for them, and re-layouts  3.93 us (5%)
  other arithmetic  1.6 us (2%)
    pallas_call x1, Pallas kernels, on_device(): pl.pallas_call(kernel, out_shape=tuple((jax.ShapeDtypeStruct((rows // k,...  27.1 us
    ppermute x6, waiting for transfers between devices, shifted(): return lax.ppermute(array, axis, pairs)  25.2 us
    ppermute x6, starting transfers between devices, shifted(): return lax.ppermute(array, axis, pairs)  17.2 us
  transfers between devices with their start and end apart: 6, of which 4 were waited for; matrix products, arithmetic and copies ran while one was open for 2% of the time, Pallas kernels for 0%

commit v1 on v0

--- a/solution.py
+++ b/solution.py
@@ -18,11 +18,9 @@
     return pltpu.roll(x, x.shape[0] - k, 0)
 
 
-def group_extremes(load_hi, load_lo, out_hi, out_lo, rows):
-    size = 128
-
+def group_extremes(load_hi, load_lo, out_hi, out_lo, rows, size=128):
     def body(c, carry):
-        r = pl.multiple_of(c * size, size)
+        r = pl.multiple_of(c * size, 8)
         top = load_hi(r, size + 8)
         if load_lo is None:
             after = rolled(top, 1)
@@ -80,9 +78,21 @@
     lax.fori_loop(0, total // size, body, 0)
 
 
-def horizontal_pass(x, vhi, vlo, relief, thi, tlo, mhi, mlo, mid, rb, strips):
+def halo_pass(x, b, start, vhi, vlo, mhi, mlo):
+    row = lambda r: pl.multiple_of(start + r, 8)
+    span = LANES + 2 * REACH - 8
+    load = lambda r, n: x[b, pl.ds(row(r), n), :]
+    group_extremes(load, None, mhi, mlo, span, span // 3)
+    last = lambda k: x[b, pl.ds(row(k * 8), 8), :]
+    for m, v, pick in ((mhi, vhi, jnp.maximum), (mlo, vlo, jnp.minimum)):
+        load = lambda k: m[k * 8 : k * 8 + 8, :]
+        for g, value in enumerate(window_chunk(load, last, pick, LANES // 8)):
+            v[b, pl.ds(row(g * 8), 8), :] = value
+
+
+def horizontal_pass(x, vhi, vlo, relief, thi, tlo, mhi, mlo, mid, start, strips):
     width = strips * LANES
-    r = pl.multiple_of(rb * LANES, LANES)
+    r = pl.multiple_of(start, 8)
     for b in range(strips):
         thi[b * LANES : (b + 1) * LANES, :] = vhi[b, pl.ds(r, LANES), :].T
         tlo[b * LANES : (b + 1) * LANES, :] = vlo[b, pl.ds(r, LANES), :].T
@@ -193,66 +203,226 @@
         store(out, total)
 
 
+def order_of(chunks):
+    order = []
+    for k in range(chunks // 2):
+        order += [chunks - 1 - k, k]
+    return order
+
+
+def blocks_of(rows):
+    chunks = rows // LANES
+    order = order_of(chunks)
+    starts = [k * LANES for k in range(chunks)] + [rows + 16 - LANES]
+    plan = []
+    for start in starts:
+        low, high = start - HALO, start + LANES + 2 * REACH - HALO
+        need = {min(max(c, 0), chunks - 1) for c in range(low // LANES, -(-high // LANES))}
+        plan.append((max(2, 1 + max(order.index(c) for c in need)), start))
+    return sorted(plan)
+
+
+def pick_by(step, values):
+    result = jnp.int32(values[0])
+    for k in range(1, len(values)):
+        result = jnp.where(step == k, jnp.int32(values[k]), result)
+    return result
+
+
 def kernel(
-    own, left, right, top, bottom, out_shade, out_first, out_second, out_third,
-    x, vhi, vlo, relief, shade, first, second, thi, tlo, mhi, mlo, mid, uhi, ulo, sems,
+    own, out_shade, out_first, out_second, out_third,
+    x, vhi, vlo, relief, shade, first, second, thi, tlo, mhi, mlo, mid, uhi, ulo,
+    sems, send_side, recv_side, send_row, recv_row, send_end, recv_end,
 ):
     rows, cols = own.shape
     strips = cols // LANES + 2
     i, ni = lax.axis_index("rows"), lax.axis_size("rows")
     j, nj = lax.axis_index("cols"), lax.axis_size("cols")
     edges = (i == 0, i == ni - 1, j == 0, j == nj - 1)
+    has = (i > 0, i < ni - 1, j > 0, j < nj - 1)
+    places = ((i - 1, j), (i + 1, j), (i, j - 1), (i, j + 1))
     mine = pl.ds(HALO, rows)
-    copies = []
-    for b in range(strips - 2):
-        copies.append((own.at[:, pl.ds(b * LANES, LANES)], x.at[b + 1, mine, :]))
-    copies.append((left, x.at[0, mine, :]))
-    copies.append((right, x.at[strips - 1, mine, :]))
-    for b in range(strips):
-        lanes = pl.ds(b * LANES, LANES)
-        copies.append((top.at[:, lanes], x.at[b, pl.ds(0, HALO), :]))
-        copies.append((bottom.at[:, lanes], x.at[b, pl.ds(HALO + rows, HALO), :]))
-    started = [pltpu.make_async_copy(s, d, sems.at[n]) for n, (s, d) in enumerate(copies)]
-    for copy in started:
+    end = HALO + rows
+    chunks = rows // LANES
+    order = order_of(chunks)
+    MESH = pl.DeviceIdType.MESH
+
+    local = []
+    for b in (0, strips - 3, *range(1, strips - 3)):
+        copy = pltpu.make_async_copy(
+            own.at[:, pl.ds(b * LANES, LANES)], x.at[b + 1, mine, :], sems.at[b]
+        )
         copy.start()
+        local.append(copy)
+
+    barrier = pltpu.get_barrier_semaphore()
+    for there, place in zip(has, places):
+
+        @pl.when(there)
+        def _():
+            pl.semaphore_signal(barrier, inc=1, device_id=place, device_id_type=MESH)
+
     mid[...] = jnp.zeros_like(mid)
-    for copy in started:
+    peers = sum(jnp.where(there, jnp.int32(1), jnp.int32(0)) for there in has)
+    pl.semaphore_wait(barrier, peers)
+
+    def side_copy(side, k):
+        at = pl.ds(HALO + order[k] * LANES, LANES)
+        source, target = ((1, strips - 1), (strips - 2, 0))[side]
+        return pltpu.make_async_remote_copy(
+            src_ref=x.at[source, at, :],
+            dst_ref=x.at[target, at, :],
+            send_sem=send_side.at[side, k],
+            recv_sem=recv_side.at[side, k],
+            device_id=places[2 + side],
+            device_id_type=MESH,
+        )
+
+    def row_copy(side):
+        source, target = ((HALO, end), (rows, 0))[side]
+        return pltpu.make_async_remote_copy(
+            src_ref=x.at[pl.ds(1, strips - 2), pl.ds(source, HALO), :],
+            dst_ref=x.at[pl.ds(1, strips - 2), pl.ds(target, HALO), :],
+            send_sem=send_row.at[side],
+            recv_sem=recv_row.at[side],
+            device_id=places[side],
+            device_id_type=MESH,
+        )
+
+    def end_copy(side, strip):
+        source, target = ((HALO, end), (rows, 0))[side]
+        b = (0, strips - 1)[strip]
+        return pltpu.make_async_remote_copy(
+            src_ref=x.at[b, pl.ds(source, HALO), :],
+            dst_ref=x.at[b, pl.ds(target, HALO), :],
+            send_sem=send_end.at[side, strip],
+            recv_sem=recv_end.at[side, strip],
+            device_id=places[side],
+            device_id_type=MESH,
+        )
+
+    local[0].wait()
+    local[1].wait()
+    for k in range(chunks):
+        for side in (0, 1):
+
+            @pl.when(has[2 + side])
+            def _():
+                side_copy(side, k).start()
+
+    for copy in local[2:]:
         copy.wait()
+    for side in (0, 1):
+
+        @pl.when(has[side])
+        def _():
+            row_copy(side).start()
+
+    for side in (0, 1):
+
+        @pl.when(has[1 - side])
+        def _():
+            row_copy(side).wait_recv()
+
+    def spread_rows(top, strip_list):
+        for b in strip_list:
+            if top:
+                x[b, 0:HALO, :] = jnp.broadcast_to(x[b, HALO : HALO + 1, :], (HALO, LANES))
+            else:
+                x[b, end : end + HALO, :] = jnp.broadcast_to(
+                    x[b, end - 1 : end, :], (HALO, LANES)
+                )
+
+    for top in (0, 1):
+
+        @pl.when(edges[1 - top])
+        def _():
+            spread_rows(top, range(1, strips - 1))
+
+    tall = rows + 2 * HALO
 
     @pl.when(edges[2])
     def _():
-        x[0, 0 : rows + 2 * HALO, :] = jnp.broadcast_to(
-            x[1, 0 : rows + 2 * HALO, 0:1], (rows + 2 * HALO, LANES)
-        )
+        x[0, 0:tall, :] = jnp.broadcast_to(x[1, 0:tall, 0:1], (tall, LANES))
 
     @pl.when(edges[3])
     def _():
-        x[strips - 1, 0 : rows + 2 * HALO, :] = jnp.broadcast_to(
-            x[strips - 2, 0 : rows + 2 * HALO, LANES - 1 : LANES], (rows + 2 * HALO, LANES)
-        )
-
-    @pl.when(edges[0])
-    def _():
-        for b in range(strips):
-            x[b, 0:HALO, :] = jnp.broadcast_to(x[b, HALO : HALO + 1, :], (HALO, LANES))
-
-    @pl.when(edges[1])
-    def _():
-        end = HALO + rows
-        for b in range(strips):
-            x[b, end : end + HALO, :] = jnp.broadcast_to(x[b, end - 1 : end, :], (HALO, LANES))
+        x[strips - 1, 0:tall, :] = jnp.broadcast_to(
+            x[strips - 2, 0:tall, LANES - 1 : LANES], (tall, LANES)
+        )
 
     def down(b, carry):
         vertical_pass(x, vhi, vlo, mhi, mlo, b, rows)
         return carry
 
-    lax.fori_loop(0, strips, down, 0)
-
-    def along(rb, carry):
-        horizontal_pass(x, vhi, vlo, relief, thi, tlo, mhi, mlo, mid, rb, strips)
-        return carry
-
-    lax.fori_loop(0, rows // LANES + 1, along, 0)
+    lax.fori_loop(1, strips - 1, down, 0)
+
+    def arrival(k):
+        for side in (0, 1):
+
+            @pl.when(has[3 - side])
+            def _():
+                side_copy(side, k).wait_recv()
+
+    arrival(0)
+    arrival(1)
+    for strip, b in ((0, 0), (1, strips - 1)):
+
+        @pl.when(has[2 + strip])
+        def _():
+            for side in (0, 1):
+
+                @pl.when(has[side])
+                def _():
+                    end_copy(side, strip).start()
+
+                @pl.when(edges[side])
+                def _():
+                    spread_rows(1 - side, (b,))
+
+    for strip in (0, 1):
+
+        @pl.when(has[2 + strip])
+        def _():
+            for side in (0, 1):
+
+                @pl.when(has[1 - side])
+                def _():
+                    end_copy(side, strip).wait_recv()
+
+    plan = blocks_of(rows)
+
+    def block(step, carry):
+        for k in range(2, chunks):
+            at = min(n for n, (need, start) in enumerate(plan) if need > k)
+
+            @pl.when(step == at)
+            def _():
+                arrival(k)
+
+        start = pick_by(step, [start for need, start in plan])
+        for b in (0, strips - 1):
+            halo_pass(x, b, start, vhi, vlo, mhi, mlo)
+        horizontal_pass(x, vhi, vlo, relief, thi, tlo, mhi, mlo, mid, start, strips)
+        return carry
+
+    lax.fori_loop(0, len(plan), block, 0)
+
+    for side in (0, 1):
+
+        @pl.when(has[2 + side])
+        def _():
+            for k in range(chunks):
+                side_copy(side, k).wait_send()
+
+        @pl.when(has[side])
+        def _():
+            row_copy(side).wait_send()
+            for strip in (0, 1):
+
+                @pl.when(has[2 + strip])
+                def _():
+                    end_copy(side, strip).wait_send()
 
     repair(relief, strips, HALO, rows, HALO - 8, HALO + rows + 8, edges)
     shade_rows(relief, shade, strips, rows)
@@ -297,7 +467,7 @@
 
     def keep_third(out, value):
         n = min(LANES, cols // 8 - (out - 1) * LANES)
-        out_third[:, (out - 1) * LANES : (out - 1) * LANES + n] = value[:, :n]
+        out_third[(out - 1) * LANES : (out - 1) * LANES + n, :] = value.T[:n, :]
 
     outs3 = range(1, 1 + -(-cols // 1024))
     next_level(second, strips2, HALO // 8, rows // 8, outs3, uhi, ulo, keep_third)
@@ -305,35 +475,19 @@
         copy.wait()
 
 
-def shifted(array, axis, by):
-    count = lax.axis_size(axis)
-    pairs = [(k, k + by) for k in range(count) if 0 <= k + by < count]
-    return lax.ppermute(array, axis, pairs)
-
-
 def on_device(terrain):
     rows, cols = terrain.shape
     strips = cols // LANES + 2
-    left = shifted(terrain[:, cols - HALO :], "cols", 1)
-    right = shifted(terrain[:, :HALO], "cols", -1)
-    top_mine = shifted(terrain[rows - HALO :], "rows", 1)
-    bottom_mine = shifted(terrain[:HALO], "rows", -1)
-    ends = jnp.concatenate([left[rows - HALO :], right[rows - HALO :]], axis=1)
-    starts = jnp.concatenate([left[:HALO], right[:HALO]], axis=1)
-    top_ends = shifted(ends, "rows", 1)
-    bottom_ends = shifted(starts, "rows", -1)
-    top = jnp.concatenate([top_ends[:, :LANES], top_mine, top_ends[:, LANES:]], axis=1)
-    bottom = jnp.concatenate([bottom_ends[:, :LANES], bottom_mine, bottom_ends[:, LANES:]], axis=1)
+    chunks = rows // LANES
     f32 = jnp.float32
     tall = rows + 2 * HALO + 8
     anywhere = pl.BlockSpec(memory_space=pl.ANY)
     vmem = pl.BlockSpec(memory_space=pltpu.VMEM)
-    return pl.pallas_call(
+    shapes = [(rows // k, cols // k) for k in (1, 2, 4)] + [(cols // 8, rows // 8)]
+    shade, first, second, third = pl.pallas_call(
         kernel,
-        out_shape=tuple(
-            jax.ShapeDtypeStruct((rows // k, cols // k), f32) for k in (1, 2, 4, 8)
-        ),
-        in_specs=[anywhere] * 5,
+        out_shape=tuple(jax.ShapeDtypeStruct(shape, f32) for shape in shapes),
+        in_specs=[anywhere],
         out_specs=(anywhere, anywhere, anywhere, vmem),
         scratch_shapes=[
             pltpu.VMEM((strips, tall, LANES), f32),
@@ -350,10 +504,19 @@
             pltpu.VMEM((strips * LANES, LANES), f32),
             pltpu.VMEM((strips, rows // 2 + 16, LANES), jnp.bfloat16),
             pltpu.VMEM((strips, rows // 2 + 16, LANES), jnp.bfloat16),
-            pltpu.SemaphoreType.DMA((3 * strips + 8,)),
+            pltpu.SemaphoreType.DMA((2 * strips,)),
+            pltpu.SemaphoreType.DMA((2, chunks)),
+            pltpu.SemaphoreType.DMA((2, chunks)),
+            pltpu.SemaphoreType.DMA((2,)),
+            pltpu.SemaphoreType.DMA((2,)),
+            pltpu.SemaphoreType.DMA((2, 2)),
+            pltpu.SemaphoreType.DMA((2, 2)),
         ],
-        compiler_params=pltpu.CompilerParams(vmem_limit_bytes=58 * 1024 * 1024),
-    )(terrain, left, right, top, bottom)
+        compiler_params=pltpu.CompilerParams(
+            collective_id=0, has_side_effects=True, vmem_limit_bytes=58 * 1024 * 1024
+        ),
+    )(terrain)
+    return shade, first, second, third.T
 
 
 def solution(mesh):

time: 76.9 us -> 52.2 us (0.68); the launches traced: 75.8 us -> 52 us
  waiting for transfers between devices: 25.2 us -> 0 us
  Pallas kernels: 27.1 us -> 46.2 us
  starting transfers between devices: 17.2 us -> 0 us
  other arithmetic: 1.6 us -> 0 us
  local copies, waits for them, and re-layouts: 3.93 us -> 5.22 us
    ppermute x6 -> x0, waiting for transfers between devices: 25.2 us -> none  [shifted(): return lax.ppermute(array, axis, pairs)]
    pallas_call x1, Pallas kernels: 27.1 us -> 46.2 us  [on_device(): pl.pallas_call(kernel, out_shape=tuple((jax.ShapeDtypeStruct(shape, f32)...]
    ppermute x6 -> x0, starting transfers between devices: 17.2 us -> none  [shifted(): return lax.ppermute(array, axis, pairs)]
    unnamed x4 -> x10, local copies, waits for them, and re-layouts: 0.01 us -> 5.22 us
    slice x6 -> x0, local copies, waits for them, and re-layouts: 2.39 us -> none  [the longest x1 1.28 us: on_device(): right = shifted(terrain[:, :HALO], 'cols', -1)]
    concatenate x4 -> x0, other arithmetic: 1.6 us -> none  [the longest x1 0.79 us: on_device(): jnp.concatenate([bottom_ends[:, :LANES], bottom_mine, bottom_ends[:, LANE...]
    pallas_call x1 -> x0, local copies, waits for them, and re-layouts: 1.54 us -> none  [on_device(): pl.pallas_call(kernel, out_shape=tuple((jax.ShapeDtypeStruct((rows // k,...]
  transfers between devices with their start and end apart: 6 -> 0, of which waited for: 4 -> 0; matrix products, arithmetic and copies ran while one was open for 2% -> 0% of each run, Pallas kernels for 0% -> 0%
where the time goes in v1:
time: 52.2 us; the launch traced here: 52 us
  Pallas kernels  46.2 us (89%)
  local copies, waits for them, and re-layouts  5.22 us (10%)
  between operations  0.66 us (1%)
    pallas_call x1, Pallas kernels, on_device(): pl.pallas_call(kernel, out_shape=tuple((jax.ShapeDtypeStruct(shape, f32)...  46.2 us
    unnamed x10, local copies, waits for them, and re-layouts  5.22 us

profile of v1, /device:TPU:19, one launch (start us, length us, event | category | flops | bytes accessed | tf_op | source)
XLA Modules:
  0.0 52.0 jit_solution(7938177327781216717)
XLA Ops:
  0.6 46.2 %shard_map.46 = (f32[1024,512]{1,0:T(8,128)}, f32[512,256]{1,0:T(8,128)}, f32[256,128]{1,0:T(8,128)}, f32[64,128]{1,0:T(8,128)}) custom-call(f32[1024,512]{1,0:T(8,128)} %own.1), custom_call_target="tpu_custom_call" | custom-call | tf_op jit(solution)/shard_map/pallas_call | solution.py:487
  46.8 0.0 copy-start
  46.8 0.0 copy-start.1
  46.8 0.0 copy-start.2
  46.8 3.1 %copy.9 = f32[1024,512]{1,0:T(8,128)} copy(f32[1024,512]{1,0:T(8,128)} %get-tuple-element.16) | data formatting | bytes 4194304
  50.0 0.0 copy-done
  50.0 0.8 %copy.10 = f32[512,256]{1,0:T(8,128)} copy(f32[512,256]{1,0:T(8,128)S(1)} %copy-done) | data formatting | bytes 1048576
  50.8 0.0 copy-done.1
  50.8 0.7 %copy.11 = f32[256,128]{1,0:T(8,128)} copy(f32[256,128]{1,0:T(8,128)S(1)} %copy-done.1) | data formatting | bytes 262144
  51.4 0.0 copy-done.2
  51.4 0.6 %copy.12 = f32[128,64]{0,1:T(8,128)} copy(f32[128,64]{0,1:T(8,128)S(1)} %bitcast.1) | data formatting | bytes 65536
Async XLA Ops:
  46.8 3.2 %copy-start = (f32[512,256]{1,0:T(8,128)S(1)}, f32[512,256]{1,0:T(8,128)}, u32[]{:S(2)}) copy-start(f32[512,256]{1,0:T(8,128)} %get-tuple-element.17) | copy-start | bytes 1572868
  46.8 4.0 %copy-start.1 = (f32[256,128]{1,0:T(8,128)S(1)}, f32[256,128]{1,0:T(8,128)}, u32[]{:S(2)}) copy-start(f32[256,128]{1,0:T(8,128)} %get-tuple-element.18) | copy-start | bytes 393220
  46.8 4.6 %copy-start.2 = (f32[64,128]{1,0:T(8,128)S(1)}, f32[64,128]{1,0:T(8,128)}, u32[]{:S(2)}) copy-start(f32[64,128]{1,0:T(8,128)} %get-tuple-element.11) | copy-start | bytes 98308

commit v2 on v1

--- a/solution.py
+++ b/solution.py
@@ -230,8 +230,7 @@
 
 
 def kernel(
-    own, out_shade, out_first, out_second, out_third,
-    x, vhi, vlo, relief, shade, first, second, thi, tlo, mhi, mlo, mid, uhi, ulo,
+    own, out_relief, x, vhi, vlo, relief, thi, tlo, mhi, mlo, mid,
     sems, send_side, recv_side, send_row, recv_row, send_end, recv_end,
 ):
     rows, cols = own.shape
@@ -407,6 +406,9 @@
         return carry
 
     lax.fori_loop(0, len(plan), block, 0)
+    some = pl.ds(HALO - 8, rows + 16)
+    away = pltpu.make_async_copy(relief.at[:, some, :], out_relief, sems.at[strips])
+    away.start()
 
     for side in (0, 1):
 
@@ -424,6 +426,23 @@
                 def _():
                     end_copy(side, strip).wait_send()
 
+    away.wait()
+
+
+def finish(
+    in_relief, out_shade, out_first, out_second, out_third,
+    relief, shade, first, second, uhi, ulo, sems,
+):
+    rows, cols = out_shade.shape
+    strips = cols // LANES + 2
+    i, ni = lax.axis_index("rows"), lax.axis_size("rows")
+    j, nj = lax.axis_index("cols"), lax.axis_size("cols")
+    edges = (i == 0, i == ni - 1, j == 0, j == nj - 1)
+    mine = pl.ds(HALO, rows)
+    some = pl.ds(HALO - 8, rows + 16)
+    fetch = pltpu.make_async_copy(in_relief, relief.at[:, some, :], sems.at[0])
+    fetch.start()
+    fetch.wait()
     repair(relief, strips, HALO, rows, HALO - 8, HALO + rows + 8, edges)
     shade_rows(relief, shade, strips, rows)
     repair(shade, strips, HALO, rows, HALO - 8, HALO + rows + 8, edges)
@@ -483,27 +502,23 @@
     tall = rows + 2 * HALO + 8
     anywhere = pl.BlockSpec(memory_space=pl.ANY)
     vmem = pl.BlockSpec(memory_space=pltpu.VMEM)
-    shapes = [(rows // k, cols // k) for k in (1, 2, 4)] + [(cols // 8, rows // 8)]
-    shade, first, second, third = pl.pallas_call(
+    strip = lambda count, tall: pltpu.VMEM((count, tall, LANES), f32)
+    params = dict(vmem_limit_bytes=58 * 1024 * 1024)
+    relief = pl.pallas_call(
         kernel,
-        out_shape=tuple(jax.ShapeDtypeStruct(shape, f32) for shape in shapes),
+        out_shape=jax.ShapeDtypeStruct((strips, rows + 16, LANES), f32),
         in_specs=[anywhere],
-        out_specs=(anywhere, anywhere, anywhere, vmem),
+        out_specs=anywhere,
         scratch_shapes=[
-            pltpu.VMEM((strips, tall, LANES), f32),
-            pltpu.VMEM((strips, rows + LANES, LANES), f32),
-            pltpu.VMEM((strips, rows + LANES, LANES), f32),
-            pltpu.VMEM((strips, tall, LANES), f32),
-            pltpu.VMEM((strips, tall, LANES), f32),
-            pltpu.VMEM((cols // 256 + 2, rows // 2 + HALO, LANES), f32),
-            pltpu.VMEM((cols // 512 + 2, rows // 4 + HALO, LANES), f32),
+            strip(strips, tall),
+            strip(strips, rows + LANES),
+            strip(strips, rows + LANES),
+            strip(strips, tall),
             pltpu.VMEM((strips * LANES + 8, LANES), f32),
             pltpu.VMEM((strips * LANES + 8, LANES), f32),
             pltpu.VMEM((max(tall, strips * LANES), LANES), f32),
             pltpu.VMEM((max(tall, strips * LANES), LANES), f32),
             pltpu.VMEM((strips * LANES, LANES), f32),
-            pltpu.VMEM((strips, rows // 2 + 16, LANES), jnp.bfloat16),
-            pltpu.VMEM((strips, rows // 2 + 16, LANES), jnp.bfloat16),
             pltpu.SemaphoreType.DMA((2 * strips,)),
             pltpu.SemaphoreType.DMA((2, chunks)),
             pltpu.SemaphoreType.DMA((2, chunks)),
@@ -513,9 +528,26 @@
             pltpu.SemaphoreType.DMA((2, 2)),
         ],
         compiler_params=pltpu.CompilerParams(
-            collective_id=0, has_side_effects=True, vmem_limit_bytes=58 * 1024 * 1024
+            collective_id=0, has_side_effects=True, **params
         ),
     )(terrain)
+    shapes = [(rows // k, cols // k) for k in (1, 2, 4)] + [(cols // 8, rows // 8)]
+    shade, first, second, third = pl.pallas_call(
+        finish,
+        out_shape=tuple(jax.ShapeDtypeStruct(shape, f32) for shape in shapes),
+        in_specs=[anywhere],
+        out_specs=(anywhere, anywhere, anywhere, vmem),
+        scratch_shapes=[
+            strip(strips, tall),
+            strip(strips, tall),
+            strip(cols // 256 + 2, rows // 2 + HALO),
+            strip(cols // 512 + 2, rows // 4 + HALO),
+            pltpu.VMEM((strips, rows // 2 + 16, LANES), jnp.bfloat16),
+            pltpu.VMEM((strips, rows // 2 + 16, LANES), jnp.bfloat16),
+            pltpu.SemaphoreType.DMA((2 * strips,)),
+        ],
+        compiler_params=pltpu.CompilerParams(**params),
+    )(relief)
     return shade, first, second, third.T
 
 

time: 52.2 us -> 50.5 us (0.967)
  local copies, waits for them, and re-layouts: 5.22 us -> 0 us
  Pallas kernels: 46.2 us -> 49.7 us
    unnamed x10 -> x0, local copies, waits for them, and re-layouts: 5.22 us -> none
    pallas_call x1 -> x2, Pallas kernels: 46.2 us -> 49.7 us  [the longest x1 35.1 us: on_device(): pl.pallas_call(kernel, out_shape=jax.ShapeDtypeStruct((strips, rows + 16,...]
where the time goes in v2:
time: 50.5 us; the launch traced here: 50.4 us
  Pallas kernels  49.7 us (98%)
  between operations  0.64 us (1%)
    pallas_call x1, Pallas kernels, on_device(): pl.pallas_call(kernel, out_shape=jax.ShapeDtypeStruct((strips, rows + 16,...  35.1 us
    pallas_call x1, Pallas kernels, on_device(): pl.pallas_call(finish, out_shape=tuple((jax.ShapeDtypeStruct(shape, f32)...  14.7 us

profile of v2, /device:TPU:19, one launch (start us, length us, event | category | flops | bytes accessed | tf_op | source)
XLA Modules:
  0.0 50.4 jit_solution(6844348699497185750)
XLA Ops:
  0.6 35.1 %shard_map.46.in_relief = f32[6,1040,128]{2,1,0:T(8,128)} custom-call(f32[1024,512]{1,0:T(8,128)} %own.1), custom_call_target="tpu_custom_call" | custom-call | tf_op jit(solution)/shard_map/pallas_call | solution.py:507
  35.7 14.7 %shard_map.47 = (f32[1024,512]{1,0:T(8,128)}, f32[512,256]{1,0:T(8,128)}, f32[256,128]{1,0:T(8,128)}, f32[64,128]{1,0:T(8,128)}) custom-call(f32[6,1040,128]{2,1,0:T(8,128)} %shard_map.46.in_relief), custom_call_target="tpu_custom_call" | custom-call | tf_op jit(solution)/shard_map/pallas_call | solution.py:535
